TPU v7x, 32 devices: a whole 2x2x4 slice. The times are simulated.
32 devices in a mesh: groups: 2 (over y), kvb: 4 (over z), tp: 4 (over x, core).
Axes of the slice: x: 2, y: 2, z: 4, core: 2. Of those that a mesh axis runs over, the one named last changes fastest.
Arguments:
- residual: bfloat16 [32, 8192], P(('groups', 'kvb')), parts along dimension 0, may hold values from -3 to 3
- queries: bfloat16 [32, 8192], P(('groups', 'kvb'), 'tp'), parts along dimension 0, may hold values from -60 to 60
- new_kv: bfloat16 [32, 2048], P(('groups', 'kvb')), parts along dimension 0, may hold values from -6 to 6
- kv_cache: bfloat16 [2048, 16, 2048], P(('groups', 'kvb', 'tp')), parts along dimension 0, may hold values from -6 to 6
- lengths: int32 [32], P('groups'), parts along dimension 0, may hold values from 1 to 2048, as said below
- slot_seq: int32 [2048], P(('groups', 'kvb', 'tp')), parts along dimension 0, may hold values from 0 to 15, as said below
- slot_block: int32 [2048], P(('groups', 'kvb', 'tp')), parts along dimension 0, may hold values from 0 to 127, as said below
- block_counts: int32 [32], P(('groups', 'kvb', 'tp')), parts along dimension 0, may hold values from 16 to 64, as said below
- out_weight: bfloat16 [8192, 8192], P('tp'), may hold values from -0.5 to 0.5
- norm_gain: bfloat16 [8192], P('tp'), may hold values from 0.099609375 to 1.8984375
Outputs:
- stream: bfloat16 [32, 8192], P(('groups', 'kvb'), 'tp'), parts along dimension 0
- normed: bfloat16 [32, 8192], P(('groups', 'kvb'), 'tp'), parts along dimension 0
There are 2 independent parts, one for each index of `groups`. A program takes and returns all parts, laid end to end along the dimension named above; an argument that names none is the same for every part. Nothing has to cross between parts.
Inputs may be any that keep to these rules, and one draw needn't show every extreme that they name: `block_counts`: slots below a device's count hold cache blocks, those at or beyond it none; at least one device's count is 64. `slot_seq`: each pair of a sequence s and a block b below ceil(lengths[s] / 16) sits in exactly one live slot of the group. `slot_block`: some sequence has exactly 128 blocks; none has more. `lengths`: some sequence has exactly 16 * (128) tokens.
All inputs are finite; a program needn't handle non-finite values.
Results may differ from a plain program's by a relative error of at most 0.006.
Values may be sent and summed in bfloat16 or wider, within the bound.
No kernel may reach another device: no remote copies, remote signals or barrier semaphores. Data moves between devices by JAX's collectives and lax.ppermute only.
A program may use at most 64 MiB of HBM per device.

v0:
```python
import jax
import jax.numpy as jnp
from jax import lax
from jax.sharding import PartitionSpec as P

QH = 64
KVH = 8
HD = 128
BLK = 16
NEGATIVE = -1e30
EPSILON = 1e-06


def on_device(
    residual,
    queries,
    new_kv,
    kv_cache,
    lengths,
    slot_seq,
    slot_block,
    block_counts,
    out_weight,
    norm_gain,
):
    tp_count = lax.axis_size("tp")
    kvb_count = lax.axis_size("kvb")
    tp_index = lax.axis_index("tp")
    seq_rep = residual.shape[0]
    local_heads = queries.shape[1] // HD
    group_size = QH // KVH
    score_scale = HD ** (-0.5)
    wide = lax.all_gather(queries, "tp", axis=1, tiled=True)
    every = lax.all_gather(wide, "kvb", axis=0, tiled=True)
    seq_total = every.shape[0]
    grouped = every.reshape(seq_total, KVH, group_size, HD)
    pool_size = kv_cache.shape[0]
    step_slots = min(32, pool_size)
    live_count = block_counts[0]
    seq_ids = jnp.arange(seq_total, dtype=jnp.int32)
    offsets = jnp.arange(BLK, dtype=jnp.int32)

    def advance(turn_index, carried):
        peak_now, weight_sum, partial_rows = carried
        first_slot = turn_index * step_slots
        cache_part = lax.dynamic_slice_in_dim(kv_cache, first_slot, step_slots, 0)
        seq_part = lax.dynamic_slice_in_dim(slot_seq, first_slot, step_slots, 0)
        block_part = lax.dynamic_slice_in_dim(slot_block, first_slot, step_slots, 0)
        key_rows = cache_part[:, :, : KVH * HD].reshape(step_slots * BLK, KVH, HD)
        value_rows = cache_part[:, :, KVH * HD :].reshape(step_slots * BLK, KVH, HD)
        token_seq = jnp.repeat(seq_part, BLK)
        position = (block_part[:, None] * BLK + offsets[None, :]).reshape(-1)
        slot_live = jnp.repeat(
            first_slot + jnp.arange(step_slots, dtype=jnp.int32) < live_count, BLK
        )
        member = token_seq[None, :] == seq_ids[:, None]
        length_of = jnp.sum(jnp.where(member, lengths[:, None], 0), axis=0)
        live = member & (position < length_of)[None, :] & slot_live[None, :]
        mask = live[:, None, None, :]
        scores = (
            jnp.einsum("sgqd,ngd->sgqn", grouped, key_rows, preferred_element_type=jnp.float32)
            * score_scale
        )
        peak_next = jnp.maximum(peak_now, jnp.max(jnp.where(mask, scores, NEGATIVE), axis=-1))
        weights = jnp.where(mask, jnp.exp(scores - peak_next[..., None]), 0.0)
        shrink = jnp.exp(peak_now - peak_next)
        weight_sum = weight_sum * shrink + jnp.sum(weights, axis=-1)
        partial_rows = partial_rows * shrink[..., None] + jnp.einsum(
            "sgqn,ngd->sgqd",
            weights.astype(jnp.bfloat16),
            value_rows,
            preferred_element_type=jnp.float32,
        )
        return (peak_next, weight_sum, partial_rows)

    start_state = (
        jnp.full((seq_total, KVH, group_size), NEGATIVE, jnp.float32),
        jnp.zeros((seq_total, KVH, group_size), jnp.float32),
        jnp.zeros((seq_total, KVH, group_size, HD), jnp.float32),
    )
    turn_count = (live_count + step_slots - 1) // step_slots
    peak_now, weight_sum, partial_rows = lax.fori_loop(0, turn_count, advance, start_state)
    row_out = partial_rows.reshape(kvb_count, seq_rep, tp_count, local_heads * HD).transpose(
        0, 2, 1, 3
    )
    peak_out = peak_now.reshape(kvb_count, seq_rep, tp_count, local_heads).transpose(0, 2, 1, 3)
    sum_out = weight_sum.reshape(kvb_count, seq_rep, tp_count, local_heads).transpose(0, 2, 1, 3)
    device_total = kvb_count * tp_count
    got_rows, got_peaks, got_sums = (
        lax.all_to_all(
            row_out.reshape(device_total, seq_rep, local_heads * HD),
            ("kvb", "tp"),
            split_axis=0,
            concat_axis=0,
            tiled=True,
        ),
        lax.all_to_all(
            peak_out.reshape(device_total, seq_rep, local_heads),
            ("kvb", "tp"),
            split_axis=0,
            concat_axis=0,
            tiled=True,
        ),
        lax.all_to_all(
            sum_out.reshape(device_total, seq_rep, local_heads),
            ("kvb", "tp"),
            split_axis=0,
            concat_axis=0,
            tiled=True,
        ),
    )
    got_rows = got_rows.reshape(device_total, seq_rep, local_heads, HD)
    kv_local = max(1, local_heads // group_size)
    per_kv = local_heads // kv_local
    kv_first = tp_index * local_heads // group_size
    new_keys = lax.dynamic_slice_in_dim(new_kv, kv_first * HD, kv_local * HD, 1).reshape(
        seq_rep, kv_local, HD
    )
    new_values = lax.dynamic_slice_in_dim(new_kv, KVH * HD + kv_first * HD, kv_local * HD, 1)
    new_values = new_values.reshape(seq_rep, kv_local, 1, HD).astype(jnp.float32)
    own_view = queries.reshape(seq_rep, kv_local, per_kv, HD)
    fresh = (
        jnp.einsum("rkqd,rkd->rkq", own_view, new_keys, preferred_element_type=jnp.float32)
        * score_scale
    )
    fresh = fresh.reshape(seq_rep, local_heads)
    fresh_values = jnp.broadcast_to(new_values, (seq_rep, kv_local, per_kv, HD)).reshape(
        seq_rep, local_heads, HD
    )
    overall = jnp.maximum(jnp.max(got_peaks, axis=0), fresh)
    scaling = jnp.exp(got_peaks - overall[None])
    fresh_weight = jnp.exp(fresh - overall)
    denominator = jnp.sum(scaling * got_sums, axis=0) + fresh_weight
    numerator = (
        jnp.sum(scaling[..., None] * got_rows, axis=0) + fresh_weight[..., None] * fresh_values
    )
    attended = (
        (numerator / denominator[..., None]).reshape(seq_rep, local_heads * HD).astype(jnp.bfloat16)
    )
    projected = jnp.dot(attended, out_weight, preferred_element_type=jnp.float32)
    width_dev = norm_gain.shape[0]
    column = tp_index * width_dev
    summed = lax.psum(projected, "tp")
    full_stream = (residual.astype(jnp.float32) + summed).astype(jnp.bfloat16)
    full_wide = lax.optimization_barrier(full_stream).astype(jnp.float32)
    mean_square = jnp.mean(full_wide * full_wide, axis=1)
    stream = lax.dynamic_slice_in_dim(full_stream, column, width_dev, 1)
    stream_wide = lax.dynamic_slice_in_dim(full_wide, column, width_dev, 1)
    normed = (
        stream_wide * lax.rsqrt(mean_square + EPSILON)[:, None] * norm_gain.astype(jnp.float32)
    ).astype(jnp.bfloat16)
    return (stream, normed)


def solution(mesh):
    placed = (
        P(("groups", "kvb"), None),
        P(("groups", "kvb"), "tp"),
        P(("groups", "kvb"), None),
        P(("groups", "kvb", "tp"), None, None),
        P("groups"),
        P(("groups", "kvb", "tp")),
        P(("groups", "kvb", "tp")),
        P(("groups", "kvb", "tp")),
        P("tp", None),
        P("tp"),
    )
    return jax.shard_map(
        on_device,
        mesh=mesh,
        in_specs=placed,
        out_specs=(P(("groups", "kvb"), "tp"), P(("groups", "kvb"), "tp")),
        check_vma=False,
    )
```

profile of v0, /device:TPU:0, one launch (start us, length us, event | category | flops | bytes accessed | tf_op | source)
XLA Modules:
  0.0 138.4 jit_solution(4578274907591061050)
XLA Ops:
  7.8 6.5 %all_gather.6 = bf16[4,8192]{1,0:T(4,128)(2,1)S(1)} all-gather(bf16[4,2048]{1,0:T(4,128)(2,1)} %param.13), channel_id=1, replica_groups=mesh['groups'=2,'kvb'=4,'tp'=4] {'tp'}, dimensions={1}, use_global_device_ids=true | all-gather | bytes 81920 | tf_op jit(solution)/shard_map/all_gather | solution.py:33
  14.3 14.5 %all-gather = bf16[4,4,8192]{2,1,0:T(4,128)(2,1)S(1)} all-gather(bf16[1,4,8192]{2,1,0:T(4,128)(2,1)S(1)} %bitcast.100), channel_id=1, replica_groups=mesh['groups'=2,'kvb'=4,'tp'=4] {'kvb'}, dimensions={0}, use_global_device_ids=true | all-gather | bytes 327680 | tf_op jit(solution)/shard_map/all_gather | solution.py:34
  28.8 0.3 reshape.180
  29.1 0.2 copy.33
  29.4 7.9 %while.17 = (s32[]{:T(128)}, f32[16,8,8]{0,2,1:T(8,128)S(1)}, f32[16,8,8]{0,2,1:T(8,128)S(1)}, f32[16,8,8,128]{3,0,2,1:T(8,128)S(1)}, s32[]{:T(128)}, /*index=5*...) while((s32[]{:T(128)}, f32[16,8,8]{0,2,1:T(8,128)S(1)}, ...), condition=%wide.region_4.5_spmd.clone.clone, body=%wide.region_0.4_spmd.clone.clone.sunk | while | flops 274516576 | bytes 18212968 | solution.py:82
  29.4 0.7 dynamic_slice.42
  30.2 0.1 eq.54
  30.3 0.7 fusion.44
  31.1 0.7 dynamic-slice_multiply_fusion.2
  31.8 0.1 iota_add_fusion.2
  31.9 0.1 add.156
  32.0 0.7 add_compare_fusion.2
  32.6 0.1 broadcast_in_dim.135
  32.7 0.1 and.71
  32.8 1.7 %constant_dynamic-slice_fusion.5 = (bf16[32,16,1024]{2,1,0:T(8,128)(2,1)S(1)}, bf16[32,16,1024]{2,1,0:T(8,128)(2,1)S(1)}) fusion(bf16[64,16,2048]{2,1,0:T(8,128)(2,1)} %get-tuple-element.348, s32[]{:T(128)S(6)} %select_n.72, s32[]{:T(128)S(6)} %add.157), kind=kLoop, calls=%fused_computation.28.clone.1 | loop fusion | bytes 4194312 | tf_op jit(solution)/shard_map/while/body/slice | solution.py:50
  34.5 0.3 copy.84
  34.8 0.6 fusion.46
  35.4 0.6 fusion.47
  36.1 0.3 copy.85
  36.3 0.9 fusion.48
  37.3 0.1 copy.34
  37.4 0.1 reshape.181
  37.5 0.6 copy.36
  38.1 12.3 %all-to-all-start = ((f32[16,4,16]{2,1,0:T(4,128)}), f32[16,4,16]{2,1,0:T(4,128)S(1)}, u32[]{:S(2)}, u32[]{:S(2)}) async-start(f32[16,4,16]{2,1,0:T(4,128)} %copy.36), calls=%async_computation | async-start | bytes 65536 | tf_op jit(solution)/shard_map/all_to_all | solution.py:97
  50.4 0.7 dynamic-slice_convert_fusion
  51.1 0.1 copy.39
  51.2 0.1 reshape.189
  51.3 0.6 copy.41
  52.0 5.1 %all-to-all-done = f32[16,4,16]{2,1,0:T(4,128)S(1)} async-done(((f32[16,4,16]{2,1,0:T(4,128)}), f32[16,4,16]{2,1,0:T(4,128)S(1)}, u32[]{:S(2)}, u32[]{:S(2)}) %all-to-all-start) | async-done | bytes 4128 | tf_op jit(solution)/shard_map/all_to_all | solution.py:97
  57.0 3.5 %all-to-all-start.2 = ((f32[16,4,16]{2,1,0:T(4,128)}), f32[16,4,16]{2,1,0:T(4,128)S(1)}, u32[]{:S(2)}, u32[]{:S(2)}) async-start(f32[16,4,16]{2,1,0:T(4,128)} %copy.41), calls=%async_computation.2 | async-start | bytes 65536 | tf_op jit(solution)/shard_map/all_to_all | solution.py:104
  60.5 0.1 fusion.26
  60.7 0.2 copy.37
  60.8 0.2 reshape.186
  61.0 1.1 copy.38
  62.2 5.0 %all-to-all-done.2 = f32[16,4,16]{2,1,0:T(4,128)S(1)} async-done(((f32[16,4,16]{2,1,0:T(4,128)}), f32[16,4,16]{2,1,0:T(4,128)S(1)}, u32[]{:S(2)}, u32[]{:S(2)}) %all-to-all-start.2) | async-done | bytes 4128 | tf_op jit(solution)/shard_map/all_to_all | solution.py:104
  67.1 3.6 %all-to-all-start.1 = ((f32[16,4,2048]{2,1,0:T(4,128)}), f32[16,4,2048]{2,1,0:T(4,128)S(1)}, u32[]{:S(2)}, u32[]{:S(2)}) async-start(f32[16,4,2048]{2,1,0:T(4,128)} %bitcast.7), calls=%async_computation.1 | async-start | bytes 1048576 | tf_op jit(solution)/shard_map/all_to_all | solution.py:90
  70.8 0.1 reshape.185
  71.0 0.2 mul.96
  71.2 0.2 mul.97
  71.4 0.1 broadcast_bitcast_fusion
  71.4 13.5 %all-to-all-done.1 = f32[16,4,2048]{2,1,0:T(4,128)S(1)} async-done(((f32[16,4,2048]{2,1,0:T(4,128)}), f32[16,4,2048]{2,1,0:T(4,128)S(1)}, u32[]{:S(2)}, u32[]{:S(2)}) %all-to-all-start.1) | async-done | bytes 524320 | tf_op jit(solution)/shard_map/all_to_all | solution.py:90
  85.0 0.1 multiply_reduce_fusion
  85.1 13.5 %fusion.24 = f32[4,8192]{1,0:T(4,128)} fusion(bf16[2048,8192]{1,0:T(8,128)(2,1)} %param.20, f32[1,4,16,128]{3,2,1,0:T(8,128)S(1)} %get-tuple-element.225, f32[4,2048]{1,0:T(4,128)S(1)} %multiply_reduce_fusion, f32[1,4,16,128]{3,2,1,0:T(8,128)S(1)} %broadcast_bitcast_fusion.1, f32[1,4,16,128]{3,2,1,0:T(8,128)S(1)} %get-tuple-element.226), kind=kOutput, calls=%fused_computation.41 | convolution fusion | flops 134250496 | bytes 33816576 | tf_op jit(solution)/shard_map/dot_general | solution.py:140
  98.7 30.4 %all-reduce.2.cloned.1.call-done = f32[4,8192]{1,0:T(4,128)} async-done(((f32[4,8192]{1,0:T(4,128)}), f32[4,8192]{1,0:T(4,128)}) %all-reduce.2.cloned.1.call-update) | async-done | bytes 131088 | tf_op jit(solution)/shard_map/psum | solution.py:143
  129.1 0.9 add_convert_fusion
  130.1 0.2 multiply_reduce_fusion.1
  130.3 0.6 constant_dynamic-slice_fusion.2
  130.9 0.7 multiply_convert_fusion
  (30 shorter events, 0.4 us)
Async XLA Ops:
  29.4 31.2 %copy-start.1 = (bf16[4,2048]{1,0:T(4,128)(2,1)S(1)}, bf16[4,2048]{1,0:T(4,128)(2,1)}, u32[]{:S(2)}) copy-start(bf16[4,2048]{1,0:T(4,128)(2,1)} %param.13) | copy-start | bytes 49156
  38.1 18.9 %all-to-all-start = ((f32[16,4,16]{2,1,0:T(4,128)}), f32[16,4,16]{2,1,0:T(4,128)S(1)}, u32[]{:S(2)}, u32[]{:S(2)}) async-start(f32[16,4,16]{2,1,0:T(4,128)} %copy.36), calls=%async_computation | async-start | bytes 65536 | tf_op jit(solution)/shard_map/all_to_all | solution.py:97
  57.0 10.1 %all-to-all-start.2 = ((f32[16,4,16]{2,1,0:T(4,128)}), f32[16,4,16]{2,1,0:T(4,128)S(1)}, u32[]{:S(2)}, u32[]{:S(2)}) async-start(f32[16,4,16]{2,1,0:T(4,128)} %copy.41), calls=%async_computation.2 | async-start | bytes 65536 | tf_op jit(solution)/shard_map/all_to_all | solution.py:104
  67.1 17.8 %all-to-all-start.1 = ((f32[16,4,2048]{2,1,0:T(4,128)}), f32[16,4,2048]{2,1,0:T(4,128)S(1)}, u32[]{:S(2)}, u32[]{:S(2)}) async-start(f32[16,4,2048]{2,1,0:T(4,128)} %bitcast.7), calls=%async_computation.1 | async-start | bytes 1048576 | tf_op jit(solution)/shard_map/all_to_all | solution.py:90
  70.7 58.4 %all-reduce.2.cloned.1.call-start = ((), (), s32[]{:S(2)}) async-start(), calls=%async_computation.3 | async-start | bytes 262144 | tf_op jit(solution)/shard_map/psum | solution.py:143
  85.1 13.6 %copy-start.2 = (bf16[2048]{0:T(1024)(128)(2,1)S(1)}, bf16[2048]{0:T(1024)(128)(2,1)}, u32[]{:S(2)}) copy-start(bf16[2048]{0:T(1024)(128)(2,1)} %param.21) | copy-start | bytes 12292
  85.1 44.0 %copy-start = (bf16[4,8192]{1,0:T(4,128)(2,1)S(1)}, bf16[4,8192]{1,0:T(4,128)(2,1)}, u32[]{:S(2)}) copy-start(bf16[4,8192]{1,0:T(4,128)(2,1)} %param.12) | copy-start | bytes 196612
Sparse Core Ops, SparseCore 0:
  98.8 30.2 all-reduce.1
where the time goes:
time: 139 us; the launch traced here: 138 us
  waiting for transfers between devices  54 us (39%)
  blocking collectives  21 us (15%)
  starting transfers between devices  19.4 us (14%)
  matrix products  15.1 us (11%)
  between operations  14.9 us (11%)
  local copies, waits for them, and re-layouts  8.16 us (6%)
  other arithmetic  5.66 us (4%)
    psum x1, waiting for transfers between devices, on_device(): summed = lax.psum(projected, 'tp')  30.4 us
    all_gather x1, blocking collectives, on_device(): every = lax.all_gather(wide, 'kvb', axis=0, tiled=True)  14.5 us
    dot_general x1, matrix products, on_device(): jnp.dot(attended, out_weight, preferred_element_type=jnp.float32)  13.5 us
    all_to_all x1, waiting for transfers between devices, on_device(): lax.all_to_all(row_out.reshape(device_total, seq_rep, local_heads * HD),...  13.5 us
    all_to_all x1, starting transfers between devices, on_device(): lax.all_to_all(peak_out.reshape(device_total, seq_rep, local_heads), ('kv...  12.3 us
    all_gather x1, blocking collectives, on_device(): wide = lax.all_gather(queries, 'tp', axis=1, tiled=True)  6.46 us
    all_to_all x1, waiting for transfers between devices, on_device(): lax.all_to_all(peak_out.reshape(device_total, seq_rep, local_heads), ('kv...  5.08 us
    all_to_all x1, waiting for transfers between devices, on_device(): lax.all_to_all(sum_out.reshape(device_total, seq_rep, local_heads), ('kvb...  4.97 us
  transfers between devices with their start and end apart: 4, of which 4 were waited for; matrix products, arithmetic and copies ran while one was open for 3% of the time, Pallas kernels for 0%

commit v1 on v0

--- a/solution.py
+++ b/solution.py
@@ -31,7 +31,12 @@
     group_size = QH // KVH
     score_scale = HD ** (-0.5)
     wide = lax.all_gather(queries, "tp", axis=1, tiled=True)
-    every = lax.all_gather(wide, "kvb", axis=0, tiled=True)
+    ring = [wide]
+    for hop in range(3):
+        ring.append(lax.ppermute(ring[-1], "kvb", [(dev, (dev + 1) % 4) for dev in range(4)]))
+    every = jnp.roll(
+        jnp.concatenate(ring[::-1], axis=0), (lax.axis_index("kvb") + 1) * ring[0].shape[0], axis=0
+    )
     seq_total = every.shape[0]
     grouped = every.reshape(seq_total, KVH, group_size, HD)
     pool_size = kv_cache.shape[0]

time: 139 us -> 139 us (level)
  waiting for transfers between devices: 54 us -> 73.9 us
  blocking collectives: 21 us -> 6.59 us
  starting transfers between devices: 19.4 us -> 15.6 us
    ppermute x0 -> x3, waiting for transfers between devices: none -> 16 us  [on_device(): lax.ppermute(ring[-1], 'kvb', [(dev, (dev + 1) % 4) for dev in range(4)])]
    all_gather x1 -> x0, blocking collectives: 14.5 us -> none  [on_device(): every = lax.all_gather(wide, 'kvb', axis=0, tiled=True)]
    all_to_all x1, starting transfers between devices: 12.3 us -> 6.43 us  [on_device(): lax.all_to_all(peak_out.reshape(device_total, seq_rep, local_heads), ('kv...]
    psum x1, waiting for transfers between devices: 30.4 us -> 34.3 us  [on_device(): summed = lax.psum(projected, 'tp')]
    ppermute x0 -> x3, starting transfers between devices: none -> 2.05 us  [on_device(): lax.ppermute(ring[-1], 'kvb', [(dev, (dev + 1) % 4) for dev in range(4)])]
  transfers between devices with their start and end apart: 4 -> 7, of which waited for: 4 -> 7; matrix products, arithmetic and copies ran while one was open for 3% -> 3% of each run, Pallas kernels for 0% -> 0%
where the time goes in v1:
time: 139 us; the launch traced here: 138 us
  waiting for transfers between devices  73.9 us (53%)
  starting transfers between devices  15.6 us (11%)
  matrix products  15.1 us (11%)
  between operations  15 us (11%)
  local copies, waits for them, and re-layouts  7.73 us (6%)
  blocking collectives  6.59 us (5%)
  other arithmetic  4.35 us (3%)
    psum x1, waiting for transfers between devices, on_device(): summed = lax.psum(projected, 'tp')  34.3 us
    ppermute x3, waiting for transfers between devices, on_device(): lax.ppermute(ring[-1], 'kvb', [(dev, (dev + 1) % 4) for dev in range(4)])  16 us
    dot_general x1, matrix products, on_device(): jnp.dot(attended, out_weight, preferred_element_type=jnp.float32)  13.5 us
    all_to_all x1, waiting for transfers between devices, on_device(): lax.all_to_all(row_out.reshape(device_total, seq_rep, local_heads * HD),...  13.5 us
    all_gather x1, blocking collectives, on_device(): wide = lax.all_gather(queries, 'tp', axis=1, tiled=True)  6.59 us
    all_to_all x1, starting transfers between devices, on_device(): lax.all_to_all(peak_out.reshape(device_total, seq_rep, local_heads), ('kv...  6.43 us
    all_to_all x1, waiting for transfers between devices, on_device(): lax.all_to_all(peak_out.reshape(device_total, seq_rep, local_heads), ('kv...  5.08 us
    all_to_all x1, waiting for transfers between devices, on_device(): lax.all_to_all(sum_out.reshape(device_total, seq_rep, local_heads), ('kvb...  4.96 us
  transfers between devices with their start and end apart: 7, of which 7 were waited for; matrix products, arithmetic and copies ran while one was open for 3% of the time, Pallas kernels for 0%

profile of v1, /device:TPU:0, one launch (start us, length us, event | category | flops | bytes accessed | tf_op | source)
XLA Modules:
  0.0 138.4 jit_solution(1293391999844865975)
XLA Ops:
  7.2 6.6 %all_gather.3 = bf16[4,8192]{1,0:T(4,128)(2,1)S(1)} all-gather(bf16[4,2048]{1,0:T(4,128)(2,1)} %param.13), channel_id=1, replica_groups=mesh['groups'=2,'kvb'=4,'tp'=4] {'tp'}, dimensions={1}, use_global_device_ids=true | all-gather | bytes 81920 | tf_op jit(solution)/shard_map/all_gather | solution.py:33
  13.8 2.0 %collective-permute-start = (bf16[4,8192]{1,0:T(4,128)(2,1)S(1)}, bf16[4,8192]{1,0:T(4,128)(2,1)S(1)}, u32[]{:S(2)}, u32[]{:S(2)}) collective-permute-start(bf16[4,8192]{1,0:T(4,128)(2,1)S(1)} %all_gather.3), channel_id=1, source_target_pairs={{0,4},{4,8},{8,12},{12,0},{1,5},{5,9},{9,13},{13,1},{2,6},{6,10},{... | collective-permute-start | bytes 196616 | tf_op jit(solution)/shard_map/ppermute | solution.py:36
  15.8 4.6 %collective-permute-done = bf16[4,8192]{1,0:T(4,128)(2,1)S(1)} collective-permute-done((bf16[4,8192]{1,0:T(4,128)(2,1)S(1)}, bf16[4,8192]{1,0:T(4,128)(2,1)S(1)}, u32[]{:S(2)}, u32[]{:S(2)}) %collective-permute-start) | collective-permute-done | bytes 65568 | tf_op jit(solution)/shard_map/ppermute | solution.py:36
  20.5 6.1 %collective-permute-done.1 = bf16[4,8192]{1,0:T(4,128)(2,1)S(1)} collective-permute-done((bf16[4,8192]{1,0:T(4,128)(2,1)S(1)}, bf16[4,8192]{1,0:T(4,128)(2,1)S(1)}, u32[]{:S(2)}, u32[]{:S(2)}) %collective-permute-start.1) | collective-permute-done | bytes 65568 | tf_op jit(solution)/shard_map/ppermute | solution.py:36
  27.2 5.4 %collective-permute-done.2 = bf16[4,8192]{1,0:T(4,128)(2,1)S(1)} collective-permute-done((bf16[4,8192]{1,0:T(4,128)(2,1)S(1)}, bf16[4,8192]{1,0:T(4,128)(2,1)S(1)}, u32[]{:S(2)}, u32[]{:S(2)}) %collective-permute-start.2) | collective-permute-done | bytes 65568 | tf_op jit(solution)/shard_map/ppermute | solution.py:36
  32.6 0.3 concatenate.6
  32.9 0.1 dynamic-slice_bitcast_fusion
  33.1 0.2 copy.33
  33.4 5.9 %while.17 = (s32[]{:T(128)}, f32[16,8,8]{0,2,1:T(8,128)S(1)}, f32[16,8,8]{0,2,1:T(8,128)S(1)}, f32[16,8,8,128]{3,0,2,1:T(8,128)S(1)}, s32[]{:T(128)}, /*index=5*...) while((s32[]{:T(128)}, f32[16,8,8]{0,2,1:T(8,128)S(1)}, ...), condition=%wide.region_4.5_spmd.clone.clone, body=%wide.region_0.4_spmd.clone.clone.sunk | while | flops 274516576 | bytes 18212968 | solution.py:87
  33.4 0.1 dynamic_slice.48
  33.5 0.1 eq.57
  33.6 0.1 fusion.44
  33.9 0.1 add.172
  34.0 0.7 add_compare_fusion.2
  34.7 0.1 and.79
  34.8 1.7 %constant_dynamic-slice_fusion.5 = (bf16[32,16,1024]{2,1,0:T(8,128)(2,1)S(1)}, bf16[32,16,1024]{2,1,0:T(8,128)(2,1)S(1)}) fusion(bf16[64,16,2048]{2,1,0:T(8,128)(2,1)} %get-tuple-element.348, s32[]{:T(128)S(6)} %select_n.86, s32[]{:T(128)S(6)} %add.173), kind=kLoop, calls=%fused_computation.28.clone.1 | loop fusion | bytes 4194312 | tf_op jit(solution)/shard_map/while/body/slice | solution.py:55
  36.5 0.3 copy.85
  36.8 0.6 fusion.46
  37.4 0.6 fusion.47
  38.1 0.3 copy.86
  38.4 0.9 fusion.48
  39.3 0.1 copy.34
  39.4 0.1 reshape.181
  39.5 0.6 copy.36
  40.1 6.4 %all-to-all-start = ((f32[16,4,16]{2,1,0:T(4,128)}), f32[16,4,16]{2,1,0:T(4,128)S(1)}, u32[]{:S(2)}, u32[]{:S(2)}) async-start(f32[16,4,16]{2,1,0:T(4,128)} %copy.36), calls=%async_computation | async-start | bytes 65536 | tf_op jit(solution)/shard_map/all_to_all | solution.py:102
  46.6 0.7 dynamic-slice_convert_fusion
  47.3 0.1 copy.39
  47.4 0.1 reshape.189
  47.5 0.6 copy.41
  48.1 5.1 %all-to-all-done = f32[16,4,16]{2,1,0:T(4,128)S(1)} async-done(((f32[16,4,16]{2,1,0:T(4,128)}), f32[16,4,16]{2,1,0:T(4,128)S(1)}, u32[]{:S(2)}, u32[]{:S(2)}) %all-to-all-start) | async-done | bytes 4128 | tf_op jit(solution)/shard_map/all_to_all | solution.py:102
  53.2 3.5 %all-to-all-start.2 = ((f32[16,4,16]{2,1,0:T(4,128)}), f32[16,4,16]{2,1,0:T(4,128)S(1)}, u32[]{:S(2)}, u32[]{:S(2)}) async-start(f32[16,4,16]{2,1,0:T(4,128)} %copy.41), calls=%async_computation.2 | async-start | bytes 65536 | tf_op jit(solution)/shard_map/all_to_all | solution.py:109
  56.7 0.1 fusion.26
  56.8 0.2 copy.37
  57.0 0.2 reshape.186
  57.2 1.1 copy.38
  58.3 5.0 %all-to-all-done.2 = f32[16,4,16]{2,1,0:T(4,128)S(1)} async-done(((f32[16,4,16]{2,1,0:T(4,128)}), f32[16,4,16]{2,1,0:T(4,128)S(1)}, u32[]{:S(2)}, u32[]{:S(2)}) %all-to-all-start.2) | async-done | bytes 4128 | tf_op jit(solution)/shard_map/all_to_all | solution.py:109
  63.3 3.6 %all-to-all-start.1 = ((f32[16,4,2048]{2,1,0:T(4,128)}), f32[16,4,2048]{2,1,0:T(4,128)S(1)}, u32[]{:S(2)}, u32[]{:S(2)}) async-start(f32[16,4,2048]{2,1,0:T(4,128)} %bitcast.6), calls=%async_computation.1 | async-start | bytes 1048576 | tf_op jit(solution)/shard_map/all_to_all | solution.py:95
  66.9 0.1 reshape.185
  67.1 0.2 mul.100
  67.3 0.2 mul.101
  67.6 13.5 %all-to-all-done.1 = f32[16,4,2048]{2,1,0:T(4,128)S(1)} async-done(((f32[16,4,2048]{2,1,0:T(4,128)}), f32[16,4,2048]{2,1,0:T(4,128)S(1)}, u32[]{:S(2)}, u32[]{:S(2)}) %all-to-all-start.1) | async-done | bytes 524320 | tf_op jit(solution)/shard_map/all_to_all | solution.py:95
  81.1 0.1 multiply_reduce_fusion
  81.3 13.5 %fusion.24 = f32[4,8192]{1,0:T(4,128)} fusion(bf16[2048,8192]{1,0:T(8,128)(2,1)} %param.20, f32[1,4,16,128]{3,2,1,0:T(8,128)S(1)} %get-tuple-element.225, f32[4,2048]{1,0:T(4,128)S(1)} %multiply_reduce_fusion, f32[1,4,16,128]{3,2,1,0:T(8,128)S(1)} %broadcast_bitcast_fusion.1, f32[1,4,16,128]{3,2,1,0:T(8,128)S(1)} %get-tuple-element.226), kind=kOutput, calls=%fused_computation.42 | convolution fusion | flops 134250496 | bytes 33816576 | tf_op jit(solution)/shard_map/dot_general | solution.py:145
  94.8 34.3 %all-reduce.2.cloned.1.call-done = f32[4,8192]{1,0:T(4,128)} async-done(((f32[4,8192]{1,0:T(4,128)}), f32[4,8192]{1,0:T(4,128)}) %all-reduce.2.cloned.1.call-update) | async-done | bytes 131088 | tf_op jit(solution)/shard_map/psum | solution.py:148
  129.1 0.9 add_convert_fusion
  130.1 0.2 multiply_reduce_fusion.1
  130.3 0.6 constant_dynamic-slice_fusion.2
  130.9 0.7 multiply_convert_fusion
  (43 shorter events, 0.8 us)
Async XLA Ops:
  7.2 26.2 %copy-start.2 = (s32[16]{0:T(128)S(1)}, s32[16]{0:T(128)}, u32[]{:S(2)}) copy-start(s32[16]{0:T(128)} %param.16) | copy-start | bytes 196
  7.2 26.2 %copy-start.4 = (s32[64]{0:T(128)S(1)}, s32[64]{0:T(128)}, u32[]{:S(2)}) copy-start(s32[64]{0:T(128)} %param.17) | copy-start | bytes 772
  7.2 26.2 %copy-start.5 = (s32[64]{0:T(128)S(1)}, s32[64]{0:T(128)}, u32[]{:S(2)}) copy-start(s32[64]{0:T(128)} %param.18) | copy-start | bytes 772
  13.8 6.7 %collective-permute-start = (bf16[4,8192]{1,0:T(4,128)(2,1)S(1)}, bf16[4,8192]{1,0:T(4,128)(2,1)S(1)}, u32[]{:S(2)}, u32[]{:S(2)}) collective-permute-start(bf16[4,8192]{1,0:T(4,128)(2,1)S(1)} %all_gather.3), channel_id=1, source_target_pairs={{0,4},{4,8},{8,12},{12,0},{1,5},{5,9},{9,13},{13,1},{2,6},{6,10},{... | collective-permute-start | bytes 196616 | tf_op jit(solution)/shard_map/ppermute | solution.py:36
  20.5 6.1 %collective-permute-start.1 = (bf16[4,8192]{1,0:T(4,128)(2,1)S(1)}, bf16[4,8192]{1,0:T(4,128)(2,1)S(1)}, u32[]{:S(2)}, u32[]{:S(2)}) collective-permute-start(bf16[4,8192]{1,0:T(4,128)(2,1)S(1)} %collective-permute-done), channel_id=1, source_target_pairs={{0,4},{4,8},{8,12},{12,0},{1,5},{5,9},{9,13},{13,1},{2,6},{6,10},{... | collective-permute-start | bytes 196616 | tf_op jit(solution)/shard_map/ppermute | solution.py:36
  26.5 6.1 %collective-permute-start.2 = (bf16[4,8192]{1,0:T(4,128)(2,1)S(1)}, bf16[4,8192]{1,0:T(4,128)(2,1)S(1)}, u32[]{:S(2)}, u32[]{:S(2)}) collective-permute-start(bf16[4,8192]{1,0:T(4,128)(2,1)S(1)} %collective-permute-done.1), channel_id=1, source_target_pairs={{0,4},{4,8},{8,12},{12,0},{1,5},{5,9},{9,13},{13,1},{2,6},{6,10},{... | collective-permute-start | bytes 196616 | tf_op jit(solution)/shard_map/ppermute | solution.py:36
  33.4 23.3 %copy-start.1 = (bf16[4,2048]{1,0:T(4,128)(2,1)S(1)}, bf16[4,2048]{1,0:T(4,128)(2,1)}, u32[]{:S(2)}) copy-start(bf16[4,2048]{1,0:T(4,128)(2,1)} %param.13) | copy-start | bytes 49156
  40.1 13.1 %all-to-all-start = ((f32[16,4,16]{2,1,0:T(4,128)}), f32[16,4,16]{2,1,0:T(4,128)S(1)}, u32[]{:S(2)}, u32[]{:S(2)}) async-start(f32[16,4,16]{2,1,0:T(4,128)} %copy.36), calls=%async_computation | async-start | bytes 65536 | tf_op jit(solution)/shard_map/all_to_all | solution.py:102
  53.2 10.1 %all-to-all-start.2 = ((f32[16,4,16]{2,1,0:T(4,128)}), f32[16,4,16]{2,1,0:T(4,128)S(1)}, u32[]{:S(2)}, u32[]{:S(2)}) async-start(f32[16,4,16]{2,1,0:T(4,128)} %copy.41), calls=%async_computation.2 | async-start | bytes 65536 | tf_op jit(solution)/shard_map/all_to_all | solution.py:109
  63.3 17.8 %all-to-all-start.1 = ((f32[16,4,2048]{2,1,0:T(4,128)}), f32[16,4,2048]{2,1,0:T(4,128)S(1)}, u32[]{:S(2)}, u32[]{:S(2)}) async-start(f32[16,4,2048]{2,1,0:T(4,128)} %bitcast.6), calls=%async_computation.1 | async-start | bytes 1048576 | tf_op jit(solution)/shard_map/all_to_all | solution.py:95
  66.9 62.3 %all-reduce.2.cloned.1.call-start = ((), (), s32[]{:S(2)}) async-start(), calls=%async_computation.3 | async-start | bytes 262144 | tf_op jit(solution)/shard_map/psum | solution.py:148
  81.2 13.6 %copy-start.3 = (bf16[2048]{0:T(1024)(128)(2,1)S(1)}, bf16[2048]{0:T(1024)(128)(2,1)}, u32[]{:S(2)}) copy-start(bf16[2048]{0:T(1024)(128)(2,1)} %param.21) | copy-start | bytes 12292
  81.2 47.9 %copy-start = (bf16[4,8192]{1,0:T(4,128)(2,1)S(1)}, bf16[4,8192]{1,0:T(4,128)(2,1)}, u32[]{:S(2)}) copy-start(bf16[4,8192]{1,0:T(4,128)(2,1)} %param.12) | copy-start | bytes 196612
Sparse Core Ops, SparseCore 0:
  94.9 34.1 all-reduce.1
